TPU v7x, 32 devices: a whole 2x2x4 slice. The times are simulated.
32 devices in a mesh: groups: 2 (over x), expert: 16 (over z, y, core).
Axes of the slice: x: 2, y: 2, z: 4, core: 2. Of those that a mesh axis runs over, the one named last changes fastest.
Arguments:
- tokens: bfloat16 [4096, 4096], P(('groups', 'expert')), parts along dimension 0, may hold values from -6 to 6
- router_weight: bfloat16 [4096, 128], replicated, may hold values from -0.078125 to 0.078125
- expert_ids: int32 [4096, 8], P(('groups', 'expert')), parts along dimension 0, may hold values from 0 to 127, all different within a row; in each aligned block of 128 rows (0 to 127, 128 to 255, ...) at most 9 rows name the same one
Outputs:
- expert_rows: bfloat16 [128, 288, 4096], P('expert', 'groups'), parts along dimension 1
- balance_loss: float32 [2], P('groups'), parts along dimension 0
There are 2 independent parts, one for each index of `groups`. A program takes and returns all parts, laid end to end along the dimension named above; an argument that names none is the same for every part. Nothing has to cross between parts.
Inputs may be any that keep to these rules, and one draw needn't show every extreme that they name: `expert_ids`: each row names 8 different experts; among the rows of one device no expert is named more than 9 times, a bound that some block reaches.
All inputs are finite; a program needn't handle non-finite values.
Results may differ from a plain program's by a relative error of at most 0.0012.
Values may be sent and summed in bfloat16 or wider, within the bound.
A program may use at most 128 MiB of HBM per device.

v0:
```python
import jax
import jax.numpy as jnp
from jax import lax
from jax.sharding import PartitionSpec as P

EXPERTS = 128
TOP_K = 8
CAP = 9


def on_device(tokens, router_weight, expert_ids):
    local_rows = tokens.shape[0]
    row_width = tokens.shape[1]
    logits = jnp.dot(tokens, router_weight, preferred_element_type=jnp.float32)
    probability = jax.nn.softmax(logits, axis=-1)
    gates = jax.nn.softmax(jnp.take_along_axis(logits, expert_ids, axis=1), axis=1)
    onehot = jnp.sum(
        (expert_ids[:, :, None] == jnp.arange(EXPERTS, dtype=jnp.int32)[None, None, :]).astype(
            jnp.int32
        ),
        axis=1,
    )
    before = jnp.cumsum(onehot, axis=0) - onehot
    slot_rank = jnp.take_along_axis(before, expert_ids, axis=1)
    slot_index = (expert_ids * CAP + slot_rank).reshape(-1)
    token_index = jnp.repeat(jnp.arange(local_rows, dtype=jnp.int32), TOP_K)
    slot_token = jnp.zeros((EXPERTS * CAP,), jnp.int32).at[slot_index].set(token_index)
    slot_gate = jnp.zeros((EXPERTS * CAP,), jnp.float32).at[slot_index].set(gates.reshape(-1))
    picked = tokens[slot_token]
    arrived = lax.all_to_all(
        picked.reshape(EXPERTS, CAP, row_width), "expert", split_axis=0, concat_axis=1, tiled=True
    )
    arrived_gates = lax.all_to_all(
        slot_gate.reshape(EXPERTS, CAP), "expert", split_axis=0, concat_axis=1, tiled=True
    )
    expert_rows = (arrived_gates[:, :, None] * arrived.astype(jnp.float32)).astype(jnp.bfloat16)
    expert_load = jnp.sum(onehot, axis=0).astype(jnp.float32)
    expert_mass = jnp.sum(probability, axis=0)
    token_total = jnp.float32(local_rows * lax.axis_size("expert"))
    load_all, mass_all = lax.psum((expert_load, expert_mass), "expert")
    summed = jnp.sum(load_all * mass_all)
    balance_loss = EXPERTS * summed / (token_total * token_total * TOP_K)
    return (expert_rows, balance_loss.reshape(1))


def solution(mesh):
    return jax.shard_map(
        on_device,
        mesh=mesh,
        in_specs=(P(("groups", "expert"), None), P(), P(("groups", "expert"), None)),
        out_specs=(P("expert", "groups", None), P("groups")),
        check_vma=False,
    )
```

profile of v0, /device:TPU:1, one launch (start us, length us, event | category | flops | bytes accessed | tf_op | source)
XLA Modules:
  0.0 468.7 jit_solution(513093752976975611)
XLA Ops:
  0.6 0.0 copy-start
  0.6 0.8 bitcast_or_fusion
  1.4 0.8 copy.31
  2.2 0.1 copy.32
  2.3 0.1 reshape.97
  2.4 0.2 convert_reduce_fusion
  2.7 0.2 reduce_window_sum.11
  2.8 0.0 copy-start.2
  2.9 6.8 %gather_fusion.1 = s32[1024]{0:T(1024)S(1)} fusion(s32[128,128]{1,0:T(8,128)S(1)} %sub.21, s32[1024]{0:T(1024)S(1)} %reshape.97), kind=kCustom, calls=%fused_computation.1 | custom fusion | bytes 16384 | tf_op jit(solution)/shard_map/jit(take_along_axis)/gather | solution.py:24
  9.7 0.1 reshape.100
  9.8 0.0 copy-done
  9.8 0.0 copy-done.2
  9.8 0.6 fusion.9
  10.4 0.0 copy-start.3
  10.4 7.0 %gather_fusion.2 = f32[1024]{0:T(1024)S(1)} fusion(f32[128,128]{0,1:T(8,128)S(1)} %get-tuple-element.15, s32[1024]{0:T(1024)S(1)} %reshape.97), kind=kCustom, calls=%fused_computation.2 | custom fusion | bytes 16384 | tf_op jit(solution)/shard_map/jit(take_along_axis)/gather | solution.py:16
  17.4 0.1 reshape.106
  17.6 0.0 copy-done.3
  17.6 0.1 copy.36
  17.8 0.1 reshape.113
  17.9 0.1 copy.34
  18.0 0.1 reshape.83
  18.1 4.3 scatter_custom_fusion
  22.4 0.8 all_to_all.9
  23.2 7.3 %all-to-all-start = ((f32[16,8,9]{2,1,0:T(8,128)}), f32[16,8,9]{2,1,0:T(8,128)S(1)}, u32[]{:S(2)}, u32[]{:S(2)}) async-start(f32[16,8,9]{2,1,0:T(8,128)} %all_to_all.9), calls=%async_computation | async-start | bytes 131072 | tf_op jit(solution)/shard_map/all_to_all | solution.py:33
  30.6 0.1 reshape.121
  30.7 4.3 scatter_custom_fusion.1
  35.0 7.9 %gather_fusion = bf16[1152,4096]{1,0:T(8,128)(2,1)} fusion(bf16[128,4096]{1,0:T(8,128)(2,1)S(1)} %copy-done, s32[2048]{0:T(1024)S(1)} %pad_clamp_fusion), kind=kCustom, calls=%fused_computation | custom fusion | bytes 18878976 | tf_op jit(solution)/shard_map/gather | solution.py:29
  42.9 15.1 %reshape.85 = bf16[128,9,4096]{2,1,0:T(8,128)(2,1)} reshape(bf16[1152,4096]{1,0:T(8,128)(2,1)} %gather_fusion) | data formatting | bytes 18874368 | tf_op jit(solution)/shard_map/reshape | solution.py:31
  58.0 0.0 all-to-all-done
  58.0 6.0 %all-to-all-start.1 = ((bf16[128,9,4096]{2,1,0:T(8,128)(2,1)}), bf16[128,9,4096]{2,1,0:T(8,128)(2,1)}, u32[]{:S(2)}, u32[]{:S(2)}) async-start(bf16[128,9,4096]{2,1,0:T(8,128)(2,1)} %reshape.85), calls=%async_computation.1 | async-start | bytes 33554432 | tf_op jit(solution)/shard_map/all_to_all | solution.py:30
  64.1 0.1 divide_reduce_fusion
  64.2 373.6 %all-reduce = (f32[128]{0:T(128)S(1)}, f32[128]{0:T(128)S(1)}) all-reduce(f32[128]{0:T(128)S(1)} %convert_element_type.27, f32[128]{0:T(128)S(1)} %divide_reduce_fusion), channel_id=1, replica_groups=mesh['groups'=2,'expert'=16] {'expert'}, use_global_device_ids=true, to_apply=%region_7.8 | all-reduce | flops 256 | bytes 2048 | tf_op jit(solution)/shard_map/psum | solution.py:40
  437.8 0.6 multiply_reduce_fusion
  439.1 0.1 mul.21
  439.2 0.1 copy.38
  439.3 0.0 all-to-all-done.1
  439.3 10.6 %copy.39 = f32[16,8,9,4096]{3,1,2,0:T(8,128)S(1)} copy(bf16[16,8,9,4096]{3,2,1,0:T(8,128)(2,1)} %bitcast.7) | data formatting | bytes 28311552 | tf_op jit(solution)/shard_map/convert_element_type | solution.py:36
  449.9 0.0 copy-start.1
  449.9 5.1 %fusion = bf16[8,144,4096]{2,0,1:T(8,128)(2,1)} fusion(f32[16,8,9,4096]{3,1,2,0:T(8,128)S(1)} %copy.39, f32[8,144]{0,1:T(8,128)S(1)} %copy.38), kind=kLoop, calls=%fused_computation.6 | loop fusion | flops 9437184 | bytes 28316160 | tf_op jit(solution)/shard_map/convert_element_type | solution.py:36
  455.0 12.6 %copy.40 = bf16[8,144,4096]{2,1,0:T(8,128)(2,1)} copy(bf16[8,144,4096]{2,0,1:T(8,128)(2,1)} %fusion) | data formatting | bytes 18874368
  467.6 0.0 copy-done.1
  (14 shorter events, 0.3 us)
Async XLA Ops:
  0.6 9.2 %copy-start = (bf16[128,4096]{1,0:T(8,128)(2,1)S(1)}, bf16[128,4096]{1,0:T(8,128)(2,1)}, u32[]{:S(2)}) copy-start(bf16[128,4096]{1,0:T(8,128)(2,1)} %param.3) | copy-start | bytes 3145732
  2.8 7.0 %copy-start.2 = (bf16[4096,128]{1,0:T(8,128)(2,1)S(1)}, bf16[4096,128]{1,0:T(8,128)(2,1)}, u32[]{:S(2)}) copy-start(bf16[4096,128]{1,0:T(8,128)(2,1)} %param.4) | copy-start | bytes 3145732
  10.4 7.2 %copy-start.3 = (s32[128,8]{0,1:T(8,128)S(1)}, s32[128,8]{0,1:T(8,128)}, u32[]{:S(2)}) copy-start(s32[128,8]{0,1:T(8,128)} %param.5) | copy-start | bytes 12292
  23.2 34.8 %all-to-all-start = ((f32[16,8,9]{2,1,0:T(8,128)}), f32[16,8,9]{2,1,0:T(8,128)S(1)}, u32[]{:S(2)}, u32[]{:S(2)}) async-start(f32[16,8,9]{2,1,0:T(8,128)} %all_to_all.9), calls=%async_computation | async-start | bytes 131072 | tf_op jit(solution)/shard_map/all_to_all | solution.py:33
  58.0 381.3 %all-to-all-start.1 = ((bf16[128,9,4096]{2,1,0:T(8,128)(2,1)}), bf16[128,9,4096]{2,1,0:T(8,128)(2,1)}, u32[]{:S(2)}, u32[]{:S(2)}) async-start(bf16[128,9,4096]{2,1,0:T(8,128)(2,1)} %reshape.85), calls=%async_computation.1 | async-start | bytes 33554432 | tf_op jit(solution)/shard_map/all_to_all | solution.py:30
  449.9 17.7 %copy-start.1 = (bf16[128,4096]{1,0:T(8,128)(2,1)S(1)}, bf16[128,4096]{1,0:T(8,128)(2,1)}, u32[]{:S(2)}) copy-start(bf16[128,4096]{1,0:T(8,128)(2,1)} %param.3) | copy-start | bytes 3145732
where the time goes:
time: 475 us; the launch traced here: 469 us
  blocking collectives  374 us (79%)
  local copies, waits for them, and re-layouts  71.4 us (15%)
  starting transfers between devices  13.4 us (3%)
  other arithmetic  7.14 us (2%)
    psum x1, blocking collectives, on_device(): load_all, mass_all = lax.psum((expert_load, expert_mass), 'expert')  374 us
    reshape x1, local copies, waits for them, and re-layouts, on_device(): picked.reshape(EXPERTS, CAP, row_width)  15.1 us
    unnamed x10, local copies, waits for them, and re-layouts  13.4 us
    convert_element_type x1, local copies, waits for them, and re-layouts, on_device(): arrived.astype(jnp.float32)  10.6 us
  transfers between devices with their start and end apart: 2, of which 0 were waited for; matrix products, arithmetic and copies ran while one was open for 6% of the time, Pallas kernels for 0%

commit v1 on v0

--- a/solution.py
+++ b/solution.py
@@ -1,11 +1,306 @@
+import functools
+
 import jax
 import jax.numpy as jnp
 from jax import lax
+from jax.experimental import pallas as pl
+from jax.experimental.pallas import tpu as pltpu
 from jax.sharding import PartitionSpec as P
 
 EXPERTS = 128
 TOP_K = 8
 CAP = 9
+LANES = 128
+LEFT, RIGHT, ACROSS, SIBLING = range(4)
+PIECES = 3
+
+
+def column_chunks(width):
+    tiles = width // LANES
+    side = max(1, tiles * 5 // 32)
+    main = tiles - side
+    edges = [main * i // PIECES for i in range(PIECES + 1)] + [tiles]
+    return [(a * LANES, (b - a) * LANES) for a, b in zip(edges[:-1], edges[1:])]
+
+
+def gather_kernel(n, x_ref, w_ref, ids_ref, buf, rmsg, msg, ssem, rsem, smsem, rmsem, lsem):
+    depth = n // 4
+    me = lax.axis_index("expert")
+    group = lax.axis_index("groups")
+    z, y, c = me // 4, (me // 2) % 2, me % 2
+    yp, cp = 1 - y, 1 - c
+    chunks = column_chunks(x_ref.shape[1])
+    last = len(chunks) - 1
+
+    def at(zz, yy, cc):
+        return zz * 4 + yy * 2 + cc
+
+    def ident(target):
+        return (group, target)
+
+    barrier = pltpu.get_barrier_semaphore()
+    for o in range(1, n):
+        pl.semaphore_signal(
+            barrier, inc=1, device_id=ident((me + o) % n), device_id_type=pl.DeviceIdType.MESH
+        )
+    pl.semaphore_wait(barrier, n - 1)
+
+    where = {
+        LEFT: at(z - 1, y, c),
+        RIGHT: at(z + 1, y, c),
+        ACROSS: at(z, yp, c),
+        SIBLING: at(z, y, cp),
+    }
+    exists = {LEFT: z > 0, RIGHT: z < depth - 1, ACROSS: None, SIBLING: None}
+    sent = []
+
+    def copy_of(src, k, way, own=False):
+        start, width = chunks[k]
+        cols = pl.ds(start, width)
+        source = x_ref.at[:, cols] if own else buf.at[src, :, cols]
+        return pltpu.make_async_remote_copy(
+            src_ref=source,
+            dst_ref=buf.at[src, :, cols],
+            send_sem=ssem.at[src, k, way],
+            recv_sem=rsem.at[src, k],
+            device_id=ident(where[way]),
+            device_id_type=pl.DeviceIdType.MESH,
+        )
+
+    def guarded(cond, fn):
+        if cond is None:
+            fn()
+        else:
+            pl.when(cond)(fn)
+
+    def send(src, k, way, own=False, held=None):
+        copy = copy_of(src, k, way, own)
+        guarded(exists[way], copy.start)
+        sent.append((held, way, src, k, own))
+
+    def arrived(src, k):
+        copy_of(src, k, SIBLING).wait_recv()
+
+    for k in range(last):
+        for way in (LEFT, RIGHT, ACROSS, SIBLING):
+            send(me, k, way, own=True)
+    send(me, last, ACROSS, own=True)
+    send(me, last, SIBLING, own=True)
+    keep = pltpu.make_async_copy(x_ref, buf.at[me], lsem)
+    keep.start()
+
+    rows = x_ref.shape[0]
+    logits = jnp.dot(x_ref[...], w_ref[...], preferred_element_type=jnp.float32)
+    ids = ids_ref[...]
+    lane = lax.broadcasted_iota(jnp.int32, (rows, EXPERTS), 1)
+    named = ids[:, 0:1] == lane
+    for k in range(1, TOP_K):
+        named = jnp.logical_or(named, ids[:, k : k + 1] == lane)
+    mask = jnp.where(named, 1.0, 0.0)
+    raised = jnp.exp(logits - jnp.max(logits, axis=1, keepdims=True))
+    probability = raised / jnp.sum(raised, axis=1, keepdims=True)
+    chosen = jnp.where(named, logits, -1e30)
+    picked = jnp.where(named, jnp.exp(chosen - jnp.max(chosen, axis=1, keepdims=True)), 0.0)
+    gates = picked / jnp.sum(picked, axis=1, keepdims=True)
+    r = lax.broadcasted_iota(jnp.int32, (rows, rows), 0)
+    q = lax.broadcasted_iota(jnp.int32, (rows, rows), 1)
+    lower = jnp.where(q < r, 1.0, 0.0).astype(jnp.bfloat16)
+    before = jnp.dot(lower, mask.astype(jnp.bfloat16), preferred_element_type=jnp.float32)
+    rank = jnp.where(named, before, -1.0)
+    mine = EXPERTS // n
+    msg[:, 0] = gates.T.reshape(n, mine, rows)
+    msg[:, 1] = rank.T.reshape(n, mine, rows)
+    stat_row = lax.broadcasted_iota(jnp.int32, (mine, EXPERTS), 0)
+    load = jnp.sum(mask, axis=0, keepdims=True)
+    mass = jnp.sum(probability, axis=0, keepdims=True)
+    stats = jnp.where(stat_row == 0, load, jnp.where(stat_row == 1, mass, 0.0))
+    msg[:, 2] = jnp.broadcast_to(stats[None], (n, mine, EXPERTS))
+    rmsg[me] = msg[me]
+
+    def note_of(target, source):
+        return pltpu.make_async_remote_copy(
+            src_ref=msg.at[target],
+            dst_ref=rmsg.at[source],
+            send_sem=smsem.at[target],
+            recv_sem=rmsem.at[source],
+            device_id=ident(target),
+            device_id_type=pl.DeviceIdType.MESH,
+        )
+
+    def from_side(d, way):
+        return z - d if way == RIGHT else z + d
+
+    def side_exists(d, way):
+        return z >= d if way == RIGHT else z < depth - d
+
+    def main_step(d, k):
+        for way in (LEFT, RIGHT):
+            src = at(from_side(d, way), y, c)
+            there = side_exists(d, way)
+
+            @pl.when(there)
+            def _():
+                arrived(src, k)
+                send(src, k, way, held=there)
+                send(src, k, ACROSS, held=there)
+                send(src, k, SIBLING, held=there)
+
+    def side_step(d):
+        for way in (LEFT, RIGHT):
+            there = side_exists(d, way)
+
+            pair = [at(from_side(d, way), line, c) for line in (y, yp)]
+
+            @pl.when(there)
+            def _():
+                for src in pair:
+                    arrived(src, last)
+                    send(src, last, way, held=there)
+                    send(src, last, SIBLING, held=there)
+
+    def across_step(d):
+        for k in range(last):
+            if d == 0:
+                src = at(z, yp, c)
+                arrived(src, k)
+                send(src, k, SIBLING)
+                continue
+            for way in (LEFT, RIGHT):
+                src = at(from_side(d, way), yp, c)
+                there = side_exists(d, way)
+
+                @pl.when(there)
+                def _():
+                    arrived(src, k)
+                    send(src, k, SIBLING, held=there)
+
+    for d in range(1, depth):
+        for k in range(last):
+            main_step(d, k)
+            if d == 1 and k == 0:
+                for o in range(1, n):
+                    note_of((me + o) % n, me).start()
+        if d == 1:
+            other = at(z, yp, c)
+            arrived(other, last)
+            send(other, last, SIBLING)
+            for way in (LEFT, RIGHT):
+                send(me, last, way, own=True)
+                send(other, last, way)
+        else:
+            side_step(d - 1)
+            if d == 2:
+                across_step(0)
+    across_step(1)
+    side_step(depth - 1)
+    for d in range(2, depth):
+        across_step(d)
+
+    for o in range(n // 2):
+        src = at(o // 2, o % 2, cp)
+        for k in range(last + 1):
+            arrived(src, k)
+    keep.wait()
+    for held, way, src, k, own in sent:
+        cond = exists[way]
+        both = cond if held is None else held if cond is None else jnp.logical_and(held, cond)
+        guarded(both, copy_of(src, k, way, own).wait_send)
+    for o in range(1, n):
+        note_of((me + o) % n, (me + n - o) % n).wait()
+
+
+def expand_kernel(n, scale, tok_ref, rmsg, out_ref, loss_ref, select, gate):
+    rows = tok_ref.shape[1]
+    mine, slots, block = out_ref.shape
+    windows = slots // 16
+    step = pl.program_id(0)
+
+    def sources(w):
+        return 16 * w // CAP, min(n, (16 * w + 15) // CAP + 1)
+
+    @pl.when(step == 0)
+    def _():
+        for w in range(windows):
+            first, stop = sources(w)
+            row = lax.broadcasted_iota(jnp.int32, (mine, 16, rows), 1).astype(jnp.float32)
+            total = jnp.zeros((mine * 16, 1), jnp.float32)
+            for s in range(first, stop):
+                want = row + jnp.float32(16 * w - CAP * s)
+                hit = jnp.logical_and(want >= 0.0, rmsg[s, 1][:, None, :] == want)
+                at = (s - first) * rows
+                one = jnp.where(hit, 1.0, 0.0).reshape(mine * 16, rows)
+                select[w, :, at : at + rows] = one.astype(jnp.bfloat16)
+                weight = jnp.where(hit, rmsg[s, 0][:, None, :], 0.0).reshape(mine * 16, rows)
+                total = total + jnp.sum(weight, axis=1, keepdims=True)
+            gate[w] = jnp.broadcast_to(total, (mine * 16, LANES))
+        both = rmsg[0, 2]
+        for s in range(1, n):
+            both = both + rmsg[s, 2]
+        loss = jnp.sum(both[0:1] * both[1:2], axis=1, keepdims=True) * scale
+        loss_ref[...] = jnp.broadcast_to(loss, loss_ref.shape)
+
+    cols = pl.ds(pl.multiple_of(step * block, block), block)
+    for w in range(windows):
+        first, stop = sources(w)
+        depth = (stop - first) * rows
+        tok = tok_ref[first:stop, :, cols].reshape(depth, block)
+        got = jnp.dot(select[w, :, :depth], tok, preferred_element_type=jnp.float32)
+        got = got * gate[w][:, 0:1]
+        out_ref[:, 16 * w : 16 * w + 16, :] = got.astype(jnp.bfloat16).reshape(mine, 16, block)
+
+
+def on_device_kernels(n, tokens, router_weight, expert_ids):
+    rows, width = tokens.shape
+    mine = EXPERTS // n
+    chunks = len(column_chunks(width))
+    vmem = pl.BlockSpec(memory_space=pltpu.VMEM)
+    dma = pltpu.SemaphoreType.DMA
+    gathered, notes = pl.pallas_call(
+        functools.partial(gather_kernel, n),
+        out_shape=(
+            pltpu.VMEM((n, rows, width), jnp.bfloat16),
+            pltpu.VMEM((n, 3, mine, EXPERTS), jnp.float32),
+        ),
+        in_specs=[vmem] * 3,
+        out_specs=(vmem, vmem),
+        scratch_shapes=[
+            pltpu.VMEM((n, 3, mine, EXPERTS), jnp.float32),
+            dma((n, chunks, 4)),
+            dma((n, chunks)),
+            dma((n,)),
+            dma((n,)),
+            dma(()),
+        ],
+        compiler_params=pltpu.CompilerParams(
+            collective_id=0, has_side_effects=True, vmem_limit_bytes=30 * 2**20
+        ),
+    )(tokens, router_weight, expert_ids)
+    total = rows * n
+    scale = EXPERTS / (float(total) * total * TOP_K)
+    block = 4 * LANES
+    slots = n * CAP
+    expert_rows, loss = pl.pallas_call(
+        functools.partial(expand_kernel, n, scale),
+        grid=(width // block,),
+        out_shape=(
+            jax.ShapeDtypeStruct((mine, slots, width), jnp.bfloat16),
+            jax.ShapeDtypeStruct((8, LANES), jnp.float32),
+        ),
+        in_specs=[vmem] * 2,
+        out_specs=(
+            pl.BlockSpec((mine, slots, block), lambda i: (0, 0, i)),
+            pl.BlockSpec((8, LANES), lambda i: (0, 0)),
+        ),
+        scratch_shapes=[
+            pltpu.VMEM((slots // 16, mine * 16, 3 * rows), jnp.bfloat16),
+            pltpu.VMEM((slots // 16, mine * 16, LANES), jnp.float32),
+        ],
+        compiler_params=pltpu.CompilerParams(vmem_limit_bytes=30 * 2**20),
+    )(
+        pltpu.with_memory_space_constraint(gathered, pltpu.VMEM),
+        pltpu.with_memory_space_constraint(notes, pltpu.VMEM),
+    )
+    return expert_rows, loss[0, :1]
 
 
 def on_device(tokens, router_weight, expert_ids):
@@ -44,8 +339,18 @@
 
 
 def solution(mesh):
+    n = mesh.shape["expert"]
+
+    def body(tokens, router_weight, expert_ids):
+        rows, width = tokens.shape
+        gathered = n * rows * width * 2
+        fits = gathered <= 24 * 2**20 and (EXPERTS // n) % 8 == 0 and rows == EXPERTS
+        if fits and n % 16 == 0 and width % 512 == 0:
+            return on_device_kernels(n, tokens, router_weight, expert_ids)
+        return on_device(tokens, router_weight, expert_ids)
+
     return jax.shard_map(
-        on_device,
+        body,
         mesh=mesh,
         in_specs=(P(("groups", "expert"), None), P(), P(("groups", "expert"), None)),
         out_specs=(P("expert", "groups", None), P("groups")),

time: 475 us -> 120 us (0.25); the launches traced: 469 us -> 120 us
  blocking collectives: 374 us -> 0 us
  Pallas kernels: 0 us -> 104 us
  local copies, waits for them, and re-layouts: 71.4 us -> 15.2 us
  starting transfers between devices: 13.4 us -> 0 us
  other arithmetic: 7.14 us -> 0 us
    psum x1 -> x0, blocking collectives: 374 us -> none  [on_device(): load_all, mass_all = lax.psum((expert_load, expert_mass), 'expert')]
    pallas_call x0 -> x2, Pallas kernels: none -> 104 us  [the longest x1 95.5 us: on_device_kernels(): pl.pallas_call(functools.partial(gather_kernel, n), out_shape=(pltpu.VMEM...]
    gather x9 -> x0, local copies, waits for them, and re-layouts: 22.2 us -> none  [the longest x1 7.9 us: on_device(): picked = tokens[slot_token]]
    reshape x3 -> x0, local copies, waits for them, and re-layouts: 15.3 us -> none  [the longest x1 15.1 us: on_device(): picked.reshape(EXPERTS, CAP, row_width)]
    all_to_all x2 -> x0, starting transfers between devices: 13.4 us -> none  [the longest x1 7.34 us: on_device(): lax.all_to_all(slot_gate.reshape(EXPERTS, CAP), 'expert', split_axis=0, c...]
    convert_element_type x1 -> x0, local copies, waits for them, and re-layouts: 10.6 us -> none  [on_device(): arrived.astype(jnp.float32)]
    scatter x2 -> x0, local copies, waits for them, and re-layouts: 8.63 us -> none  [the longest x1 4.32 us: on_device(): jnp.zeros((EXPERTS * CAP,), jnp.float32).at[slot_index]]
    convert_element_type x2 -> x0, other arithmetic: 5.08 us -> none  [the longest x1 5.08 us: on_device(): (arrived_gates[:, :, None] * arrived.astype(jnp.float32)).astype(jnp.bflo...]
  transfers between devices with their start and end apart: 2 -> 0, of which waited for: 0 -> 0; matrix products, arithmetic and copies ran while one was open for 6% -> 0% of each run, Pallas kernels for 0% -> 0%
where the time goes in v1:
time: 120 us
  Pallas kernels  104 us (87%)
  local copies, waits for them, and re-layouts  15.2 us (13%)
    pallas_call x1, Pallas kernels, on_device_kernels(): pl.pallas_call(functools.partial(gather_kernel, n), out_shape=(pltpu.VMEM...  95.5 us
    unnamed x9, local copies, waits for them, and re-layouts  14.7 us
    pallas_call x1, Pallas kernels, on_device_kernels(): pl.pallas_call(functools.partial(expand_kernel, n, scale), grid=(width //...  8.24 us

profile of v1, /device:TPU:1, one launch (start us, length us, event | category | flops | bytes accessed | tf_op | source)
XLA Modules:
  0.0 119.6 jit_solution(5928327648242108683)
XLA Ops:
  0.6 0.8 copy.5.ids_ref
  1.4 0.0 copy-start.2
  1.4 1.2 %copy-done.2 = bf16[128,4096]{1,0:T(8,128)(2,1)S(1)} copy-done((bf16[128,4096]{1,0:T(8,128)(2,1)S(1)}, bf16[128,4096]{1,0:T(8,128)(2,1)}, u32[]{:S(2)}) %copy-start.2) | copy-done | bytes 1048600
  2.6 0.0 copy-start.3
  2.6 1.2 %copy-done.3 = bf16[4096,128]{1,0:T(8,128)(2,1)S(1)} copy-done((bf16[4096,128]{1,0:T(8,128)(2,1)S(1)}, bf16[4096,128]{1,0:T(8,128)(2,1)}, u32[]{:S(2)}) %copy-start.3) | copy-done | bytes 1048600
  3.9 95.5 %shard_map.50 = (bf16[16,128,4096]{2,1,0:T(8,128)(2,1)S(1)}, f32[16,3,8,128]{3,2,1,0:T(8,128)S(1)}) custom-call(bf16[128,4096]{1,0:T(8,128)(2,1)S(1)} %copy-done.2, bf16[4096,128]{1,0:T(8,128)(2,1)S(1)} %copy-done.3, s32[128,8]{1,0:T(8,128)S(1)} %copy.5.ids_ref), custom_call_target="tpu_custom_call" | custom-call | tf_op jit(solution)/shard_map/pallas_call | solution.py:258
  99.4 0.0 copy-start
  99.4 5.7 %copy-done = bf16[16,128,4096]{2,1,0:T(8,128)(2,1)} copy-done((bf16[16,128,4096]{2,1,0:T(8,128)(2,1)}, bf16[16,128,4096]{2,1,0:T(8,128)(2,1)S(1)}, u32[]{:S(2)}) %copy-start) | copy-done | bytes 16777240
  105.1 0.0 copy-start.1
  105.1 5.8 %copy-done.1 = bf16[16,128,4096]{2,1,0:T(8,128)(2,1)S(1)} copy-done((bf16[16,128,4096]{2,1,0:T(8,128)(2,1)S(1)}, bf16[16,128,4096]{2,1,0:T(8,128)(2,1)}, u32[]{:S(2)}) %copy-start.1) | copy-done | bytes 16777240
  110.8 8.2 %shard_map.51 = (bf16[8,144,4096]{2,1,0:T(8,128)(2,1)}, f32[8,128]{1,0:T(8,128)S(1)}) custom-call(bf16[16,128,4096]{2,1,0:T(8,128)(2,1)S(1)} %copy-done.1, f32[16,3,8,128]{3,2,1,0:T(8,128)S(1)} %get-tuple-element.7.rmsg), custom_call_target="tpu_custom_call" | custom-call | tf_op jit(solution)/shard_map/pallas_call | solution.py:282
  119.1 0.5 slice.3
Async XLA Ops:
  1.4 1.2 %copy-start.2 = (bf16[128,4096]{1,0:T(8,128)(2,1)S(1)}, bf16[128,4096]{1,0:T(8,128)(2,1)}, u32[]{:S(2)}) copy-start(bf16[128,4096]{1,0:T(8,128)(2,1)} %x_ref.1) | copy-start | bytes 3145732
  2.6 1.2 %copy-start.3 = (bf16[4096,128]{1,0:T(8,128)(2,1)S(1)}, bf16[4096,128]{1,0:T(8,128)(2,1)}, u32[]{:S(2)}) copy-start(bf16[4096,128]{1,0:T(8,128)(2,1)} %w_ref.1) | copy-start | bytes 3145732
  99.4 5.7 %copy-start = (bf16[16,128,4096]{2,1,0:T(8,128)(2,1)}, bf16[16,128,4096]{2,1,0:T(8,128)(2,1)S(1)}, u32[]{:S(2)}) copy-start(bf16[16,128,4096]{2,1,0:T(8,128)(2,1)S(1)} %get-tuple-element.6.tok_ref) | copy-start | bytes 50331652
  105.1 5.8 %copy-start.1 = (bf16[16,128,4096]{2,1,0:T(8,128)(2,1)S(1)}, bf16[16,128,4096]{2,1,0:T(8,128)(2,1)}, u32[]{:S(2)}) copy-start(bf16[16,128,4096]{2,1,0:T(8,128)(2,1)} %copy-done) | copy-start | bytes 50331652

commit v2 on v0

--- a/solution.py
+++ b/solution.py
@@ -1,11 +1,365 @@
+import functools
+
 import jax
 import jax.numpy as jnp
 from jax import lax
+from jax.experimental import pallas as pl
+from jax.experimental.pallas import tpu as pltpu
 from jax.sharding import PartitionSpec as P
 
 EXPERTS = 128
 TOP_K = 8
 CAP = 9
+LANES = 128
+LEFT, RIGHT, ACROSS, SIBLING = range(4)
+PIECES = 3
+
+
+def column_chunks(width):
+    tiles = width // LANES
+    side = max(1, tiles * 5 // 32)
+    main = tiles - side
+    edges = [main * i // PIECES for i in range(PIECES + 1)] + [tiles]
+    return [(a * LANES, (b - a) * LANES) for a, b in zip(edges[:-1], edges[1:])]
+
+
+def dispatch_kernel(
+    n, scale, x_hbm, w_hbm, ids_ref, out_ref, loss_ref,
+    buf, w_ref, msg, notes, stat, stats, select, gate, ssem, rsem, nsem, tsem, lsem,
+):
+    depth = n // 4
+    me = lax.axis_index("expert")
+    group = lax.axis_index("groups")
+    z, y, c = me // 4, (me // 2) % 2, me % 2
+    yp, cp = 1 - y, 1 - c
+    rows, width = x_hbm.shape
+    mine, slots = out_ref.shape[:2]
+    chunks = column_chunks(width)
+    last = len(chunks) - 1
+    span = chunks[0][1]
+
+    def at(zz, yy, cc):
+        return zz * 4 + yy * 2 + cc
+
+    def ident(target):
+        return (group, target)
+
+    fetch = pltpu.make_async_copy(x_hbm, buf.at[me], lsem.at[0])
+    fetch.start()
+    fetch_w = pltpu.make_async_copy(w_hbm, w_ref, lsem.at[1])
+    fetch_w.start()
+    barrier = pltpu.get_barrier_semaphore()
+    for o in range(1, n):
+        pl.semaphore_signal(
+            barrier, inc=1, device_id=ident((me + o) % n), device_id_type=pl.DeviceIdType.MESH
+        )
+    fetch.wait()
+    pl.semaphore_wait(barrier, n - 1)
+
+    where = {
+        LEFT: at(z - 1, y, c),
+        RIGHT: at(z + 1, y, c),
+        ACROSS: at(z, yp, c),
+        SIBLING: at(z, y, cp),
+    }
+    exists = {LEFT: z > 0, RIGHT: z < depth - 1, ACROSS: None, SIBLING: None}
+    sent = []
+
+    def copy_of(src, k, way):
+        start, wide = chunks[k]
+        part = buf.at[src, :, pl.ds(start, wide)]
+        return pltpu.make_async_remote_copy(
+            src_ref=part,
+            dst_ref=part,
+            send_sem=ssem.at[src, k, way],
+            recv_sem=rsem.at[src, k],
+            device_id=ident(where[way]),
+            device_id_type=pl.DeviceIdType.MESH,
+        )
+
+    def guarded(cond, fn):
+        if cond is None:
+            fn()
+        else:
+            pl.when(cond)(fn)
+
+    def send(src, k, way, held=None):
+        guarded(exists[way], copy_of(src, k, way).start)
+        sent.append((held, way, src, k))
+
+    def arrived(src, k):
+        copy_of(src, k, SIBLING).wait_recv()
+
+    def own(k):
+        for way in (LEFT, RIGHT, ACROSS, SIBLING):
+            send(me, k, way)
+
+    own(0)
+
+    fetch_w.wait()
+    logits = jnp.dot(buf[me], w_ref[...], preferred_element_type=jnp.float32)
+    raised = jnp.exp(logits - jnp.max(logits, axis=1, keepdims=True))
+    probability = raised / jnp.sum(raised, axis=1, keepdims=True)
+    across = logits.T
+    ids = ids_ref[...]
+    expert = lax.broadcasted_iota(jnp.int32, (EXPERTS, rows), 0)
+    named = ids[0:1, :] == expert
+    for k in range(1, TOP_K):
+        named = jnp.logical_or(named, ids[k : k + 1, :] == expert)
+    mask = jnp.where(named, 1.0, 0.0)
+    chosen = jnp.where(named, across, -1e30)
+    picked = jnp.where(named, jnp.exp(chosen - jnp.max(chosen, axis=0, keepdims=True)), 0.0)
+    gates = jnp.where(named, picked / jnp.sum(picked, axis=0, keepdims=True), -1.0)
+    msg[...] = gates.reshape(n, mine, rows)
+    stat[:, :EXPERTS] = jnp.sum(mask.T, axis=0, keepdims=True)
+    stat[:, EXPERTS:] = jnp.sum(probability, axis=0, keepdims=True)
+    notes[me] = msg[me]
+    stats[me] = stat[...]
+
+    @pl.loop(0, mine)
+    def _(e):
+        out_ref[e] = jnp.zeros(out_ref.shape[1:], out_ref.dtype)
+
+    def note_of(target, source):
+        return (
+            pltpu.make_async_remote_copy(
+                src_ref=msg.at[target],
+                dst_ref=notes.at[source],
+                send_sem=nsem.at[0, target],
+                recv_sem=nsem.at[1, source],
+                device_id=ident(target),
+                device_id_type=pl.DeviceIdType.MESH,
+            ),
+            pltpu.make_async_remote_copy(
+                src_ref=stat,
+                dst_ref=stats.at[source],
+                send_sem=tsem.at[0, target],
+                recv_sem=tsem.at[1, source],
+                device_id=ident(target),
+                device_id_type=pl.DeviceIdType.MESH,
+            ),
+        )
+
+    for o in range(1, n):
+        for note in note_of((me + o) % n, me):
+            note.start()
+    for k in range(1, last):
+        own(k)
+    send(me, last, ACROSS)
+    send(me, last, SIBLING)
+
+    def from_side(d, way):
+        return z - d if way == RIGHT else z + d
+
+    def side_exists(d, way):
+        return z >= d if way == RIGHT else z < depth - d
+
+    def main_step(d, k):
+        for way in (LEFT, RIGHT):
+            src = at(from_side(d, way), y, c)
+            there = side_exists(d, way)
+
+            @pl.when(there)
+            def _():
+                arrived(src, k)
+                send(src, k, way, held=there)
+                send(src, k, ACROSS, held=there)
+                send(src, k, SIBLING, held=there)
+
+    def side_step(d):
+        for way in (LEFT, RIGHT):
+            there = side_exists(d, way)
+            pair = [at(from_side(d, way), line, c) for line in (y, yp)]
+
+            @pl.when(there)
+            def _():
+                for src in pair:
+                    arrived(src, last)
+                    send(src, last, way, held=there)
+                    send(src, last, SIBLING, held=there)
+
+    def across_step(d, k):
+        if d == 0:
+            src = at(z, yp, c)
+            arrived(src, k)
+            send(src, k, SIBLING)
+            return
+        for way in (LEFT, RIGHT):
+            src = at(from_side(d, way), yp, c)
+            there = side_exists(d, way)
+
+            @pl.when(there)
+            def _():
+                arrived(src, k)
+                send(src, k, SIBLING, held=there)
+
+    def window(src):
+        return jnp.minimum((CAP * src) // 16 * 16, slots - 32)
+
+    def build(src):
+        note = notes[src]
+        chose = note >= 0.0
+        r = lax.broadcasted_iota(jnp.int32, (rows, rows), 0)
+        q = lax.broadcasted_iota(jnp.int32, (rows, rows), 1)
+        upper = jnp.where(r < q, 1.0, 0.0).astype(jnp.bfloat16)
+        ones = jnp.where(chose, 1.0, 0.0).astype(jnp.bfloat16)
+        rank = jnp.dot(ones, upper, preferred_element_type=jnp.float32)
+        rank = jnp.where(chose, rank, -100.0)
+        row = lax.broadcasted_iota(jnp.int32, (mine, 32, rows), 1) + (window(src) - CAP * src)
+        hit = row.astype(jnp.float32) == rank[:, None, :]
+        one = jnp.where(hit, 1.0, 0.0).reshape(mine * 32, rows)
+        select[src] = one.astype(jnp.bfloat16)
+        weight = jnp.where(hit, note[:, None, :], 0.0).reshape(mine * 32, rows)
+        total = jnp.sum(weight, axis=1, keepdims=True)
+        gate[src] = jnp.broadcast_to(total, (mine * 32, LANES))
+
+    def expand(src, start, wide):
+        cols = pl.ds(start, wide)
+        win = pl.ds(pl.multiple_of(window(src), 16), 32)
+        got = jnp.dot(select[src], buf[src, :, cols], preferred_element_type=jnp.float32)
+        got = (got * gate[src][:, 0:1]).astype(jnp.bfloat16).reshape(mine, 32, wide)
+        out_ref[:, win, cols] = out_ref[:, win, cols] + got
+
+    def from_sibling(src, k):
+        pltpu.make_async_remote_copy(
+            src_ref=part_of(src, k),
+            dst_ref=part_of(src, k),
+            send_sem=ssem.at[src, k, SIBLING],
+            recv_sem=rsem.at[src, k],
+            device_id=ident(where[SIBLING]),
+            device_id_type=pl.DeviceIdType.MESH,
+        ).wait_recv()
+
+    def part_of(src, k):
+        return buf.at[src, :, pl.ds(pl.multiple_of(k * span, LANES), span)]
+
+    def fill_main(zs, line, first=0, stop=last):
+        @pl.loop(0, 2 * (stop - first))
+        def _(i):
+            k = first + i // 2
+            theirs = i % 2
+            src = at(zs, line, jnp.where(theirs == 1, cp, c))
+
+            @pl.when(theirs == 1)
+            def _():
+                from_sibling(src, k)
+
+            expand(src, pl.multiple_of(k * span, LANES), span)
+
+    def fill_side(zs):
+        start, wide = chunks[last]
+
+        @pl.loop(0, 4)
+        def _(i):
+            theirs = i % 2
+            src = at(zs, i // 2, jnp.where(theirs == 1, cp, c))
+
+            @pl.when(theirs == 1)
+            def _():
+                arrived(src, last)
+
+            expand(src, start, wide)
+
+    def fill_far(d, line, first=0, stop=last):
+        @pl.loop(0, 2)
+        def _(i):
+            zs = jnp.where(i == 0, z - d, z + d)
+
+            @pl.when(jnp.logical_and(zs >= 0, zs < depth))
+            def _():
+                fill_main(zs, line, first, stop)
+
+    def fill_side_far(d):
+        @pl.loop(0, 2)
+        def _(i):
+            zs = jnp.where(i == 0, z - d, z + d)
+
+            @pl.when(jnp.logical_and(zs >= 0, zs < depth))
+            def _():
+                fill_side(zs)
+
+    for d in range(1, depth):
+        for k in range(last):
+            main_step(d, k)
+        if d == 1:
+            other = at(z, yp, c)
+            arrived(other, last)
+            send(other, last, SIBLING)
+            for way in (LEFT, RIGHT):
+                send(me, last, way)
+                send(other, last, way)
+            for o in range(1, n):
+                for note in note_of((me + o) % n, (me + n - o) % n):
+                    note.wait()
+            pl.loop(0, n)(build)
+            fill_main(z, y)
+            fill_side(z)
+        else:
+            side_step(d - 1)
+            if d == 2:
+                for k in range(last):
+                    across_step(0, k)
+                fill_far(1, y)
+                fill_main(z, yp)
+                fill_side_far(1)
+    for d in range(2, depth):
+        fill_far(d, y)
+    for k in range(last):
+        across_step(1, k)
+    fill_far(1, yp)
+    side_step(depth - 1)
+    for d in range(2, depth):
+        fill_side_far(d)
+    both = jnp.sum(stats[...], axis=0)
+    loss_ref[0] = jnp.sum(both[:, :EXPERTS] * both[:, EXPERTS:]) * scale
+    for d in range(2, depth):
+        for k in range(last):
+            across_step(d, k)
+            fill_far(d, yp, k, k + 1)
+
+    for held, way, src, k in sent:
+        cond = exists[way]
+        both = cond if held is None else held if cond is None else jnp.logical_and(held, cond)
+        guarded(both, copy_of(src, k, way).wait_send)
+
+
+def on_device_kernels(n, tokens, router_weight, expert_ids):
+    rows, width = tokens.shape
+    mine = EXPERTS // n
+    slots = n * CAP
+    chunks = len(column_chunks(width))
+    vmem = pl.BlockSpec(memory_space=pltpu.VMEM)
+    hbm = pl.BlockSpec(memory_space=pltpu.HBM)
+    dma = pltpu.SemaphoreType.DMA
+    total = rows * n
+    scale = EXPERTS / (float(total) * total * TOP_K)
+    return pl.pallas_call(
+        functools.partial(dispatch_kernel, n, scale),
+        out_shape=(
+            pltpu.VMEM((mine, slots, width), jnp.bfloat16),
+            jax.ShapeDtypeStruct((1,), jnp.float32),
+        ),
+        in_specs=[hbm, hbm, vmem],
+        out_specs=(vmem, pl.BlockSpec(memory_space=pltpu.SMEM)),
+        scratch_shapes=[
+            pltpu.VMEM((n, rows, width), jnp.bfloat16),
+            pltpu.VMEM(router_weight.shape, jnp.bfloat16),
+            pltpu.VMEM((n, mine, rows), jnp.float32),
+            pltpu.VMEM((n, mine, rows), jnp.float32),
+            pltpu.VMEM((1, 2 * EXPERTS), jnp.float32),
+            pltpu.VMEM((n, 1, 2 * EXPERTS), jnp.float32),
+            pltpu.VMEM((n, mine * 32, rows), jnp.bfloat16),
+            pltpu.VMEM((n, mine * 32, LANES), jnp.float32),
+            dma((n, chunks, 4)),
+            dma((n, chunks)),
+            dma((2, n)),
+            dma((2, n)),
+            dma((2,)),
+        ],
+        compiler_params=pltpu.CompilerParams(
+            collective_id=0, has_side_effects=True, vmem_limit_bytes=40 * 2**20
+        ),
+    )(tokens, router_weight, expert_ids.T)
 
 
 def on_device(tokens, router_weight, expert_ids):
@@ -44,8 +398,18 @@
 
 
 def solution(mesh):
+    n = mesh.shape["expert"]
+
+    def body(tokens, router_weight, expert_ids):
+        rows, width = tokens.shape
+        gathered = n * rows * width * 2
+        fits = gathered <= 24 * 2**20 and (EXPERTS // n) % 8 == 0 and rows == EXPERTS
+        if fits and n % 16 == 0 and width % (32 * LANES) == 0:
+            return on_device_kernels(n, tokens, router_weight, expert_ids)
+        return on_device(tokens, router_weight, expert_ids)
+
     return jax.shard_map(
-        on_device,
+        body,
         mesh=mesh,
         in_specs=(P(("groups", "expert"), None), P(), P(("groups", "expert"), None)),
         out_specs=(P("expert", "groups", None), P("groups")),

time: 475 us -> 113 us (0.24); the launches traced: 469 us -> 113 us
  blocking collectives: 374 us -> 0 us
  Pallas kernels: 0 us -> 103 us
  local copies, waits for them, and re-layouts: 71.4 us -> 6.87 us
  starting transfers between devices: 13.4 us -> 0 us
  other arithmetic: 7.14 us -> 0 us
    psum x1 -> x0, blocking collectives: 374 us -> none  [on_device(): load_all, mass_all = lax.psum((expert_load, expert_mass), 'expert')]
    pallas_call x0 -> x1, Pallas kernels: none -> 103 us  [on_device_kernels(): pl.pallas_call(functools.partial(dispatch_kernel, n, scale), out_shape=(p...]
    gather x9 -> x0, local copies, waits for them, and re-layouts: 22.2 us -> none  [the longest x1 7.9 us: on_device(): picked = tokens[slot_token]]
    reshape x3 -> x0, local copies, waits for them, and re-layouts: 15.3 us -> none  [the longest x1 15.1 us: on_device(): picked.reshape(EXPERTS, CAP, row_width)]
    all_to_all x2 -> x0, starting transfers between devices: 13.4 us -> none  [the longest x1 7.34 us: on_device(): lax.all_to_all(slot_gate.reshape(EXPERTS, CAP), 'expert', split_axis=0, c...]
    convert_element_type x1 -> x0, local copies, waits for them, and re-layouts: 10.6 us -> none  [on_device(): arrived.astype(jnp.float32)]
    scatter x2 -> x0, local copies, waits for them, and re-layouts: 8.63 us -> none  [the longest x1 4.32 us: on_device(): jnp.zeros((EXPERTS * CAP,), jnp.float32).at[slot_index]]
    unnamed x10 -> x7, local copies, waits for them, and re-layouts: 13.4 us -> 6.87 us
  transfers between devices with their start and end apart: 2 -> 0, of which waited for: 0 -> 0; matrix products, arithmetic and copies ran while one was open for 6% -> 0% of each run, Pallas kernels for 0% -> 0%
where the time goes in v2:
time: 113 us
  Pallas kernels  103 us (91%)
  local copies, waits for them, and re-layouts  6.87 us (6%)
  between operations  2.39 us (2%)
    pallas_call x1, Pallas kernels, on_device_kernels(): pl.pallas_call(functools.partial(dispatch_kernel, n, scale), out_shape=(p...  103 us
    unnamed x7, local copies, waits for them, and re-layouts  6.87 us

profile of v2, /device:TPU:1, one launch (start us, length us, event | category | flops | bytes accessed | tf_op | source)
XLA Modules:
  0.0 112.7 jit_solution(15814991532788904022)
XLA Ops:
  0.6 0.0 copy-start
  0.6 1.2 %copy-done = bf16[128,4096]{1,0:T(8,128)(2,1)S(1)} copy-done((bf16[128,4096]{1,0:T(8,128)(2,1)S(1)}, bf16[128,4096]{1,0:T(8,128)(2,1)}, u32[]{:S(2)}) %copy-start) | copy-done | bytes 1048600
  1.9 0.0 copy-start.1
  1.9 1.2 %copy-done.1 = bf16[4096,128]{1,0:T(8,128)(2,1)S(1)} copy-done((bf16[4096,128]{1,0:T(8,128)(2,1)S(1)}, bf16[4096,128]{1,0:T(8,128)(2,1)}, u32[]{:S(2)}) %copy-start.1) | copy-done | bytes 1048600
  3.1 0.0 copy-start.2
  3.1 0.7 copy-done.2
  3.8 103.4 %shard_map.50 = (bf16[8,144,4096]{2,1,0:T(8,128)(2,1)S(1)}, f32[1]{0:T(128)}) custom-call(bf16[128,4096]{1,0:T(8,128)(2,1)S(1)} %copy-done, bf16[4096,128]{1,0:T(8,128)(2,1)S(1)} %copy-done.1, s32[8,128]{1,0:T(8,128)S(1)} %bitcast.1), custom_call_target="tpu_custom_call" | custom-call | tf_op jit(solution)/shard_map/pallas_call | solution.py:336
  107.2 3.7 %copy.7 = bf16[8,144,4096]{2,1,0:T(8,128)(2,1)} copy(bf16[8,144,4096]{2,1,0:T(8,128)(2,1)S(1)} %get-tuple-element.2) | data formatting | bytes 18874368
Async XLA Ops:
  0.6 1.2 %copy-start = (bf16[128,4096]{1,0:T(8,128)(2,1)S(1)}, bf16[128,4096]{1,0:T(8,128)(2,1)}, u32[]{:S(2)}) copy-start(bf16[128,4096]{1,0:T(8,128)(2,1)} %x_hbm.1) | copy-start | bytes 3145732
  1.9 1.2 %copy-start.1 = (bf16[4096,128]{1,0:T(8,128)(2,1)S(1)}, bf16[4096,128]{1,0:T(8,128)(2,1)}, u32[]{:S(2)}) copy-start(bf16[4096,128]{1,0:T(8,128)(2,1)} %w_hbm.1) | copy-start | bytes 3145732
  3.1 0.7 copy-start.2

commit v3 on v2

--- a/solution.py
+++ b/solution.py
@@ -193,31 +193,35 @@
                 arrived(src, k)
                 send(src, k, SIBLING, held=there)
 
-    def window(src):
-        return jnp.minimum((CAP * src) // 16 * 16, slots - 32)
-
-    def build(src):
-        note = notes[src]
-        chose = note >= 0.0
+    def window(chip):
+        return jnp.minimum((2 * CAP * chip) // 16 * 16, slots - 32)
+
+    def build(chip):
         r = lax.broadcasted_iota(jnp.int32, (rows, rows), 0)
         q = lax.broadcasted_iota(jnp.int32, (rows, rows), 1)
         upper = jnp.where(r < q, 1.0, 0.0).astype(jnp.bfloat16)
-        ones = jnp.where(chose, 1.0, 0.0).astype(jnp.bfloat16)
-        rank = jnp.dot(ones, upper, preferred_element_type=jnp.float32)
-        rank = jnp.where(chose, rank, -100.0)
-        row = lax.broadcasted_iota(jnp.int32, (mine, 32, rows), 1) + (window(src) - CAP * src)
-        hit = row.astype(jnp.float32) == rank[:, None, :]
-        one = jnp.where(hit, 1.0, 0.0).reshape(mine * 32, rows)
-        select[src] = one.astype(jnp.bfloat16)
-        weight = jnp.where(hit, note[:, None, :], 0.0).reshape(mine * 32, rows)
-        total = jnp.sum(weight, axis=1, keepdims=True)
-        gate[src] = jnp.broadcast_to(total, (mine * 32, LANES))
-
-    def expand(src, start, wide):
+        total = jnp.zeros((mine * 32, 1), jnp.float32)
+        for core in range(2):
+            src = 2 * chip + core
+            note = notes[src]
+            chose = note >= 0.0
+            ones = jnp.where(chose, 1.0, 0.0).astype(jnp.bfloat16)
+            rank = jnp.dot(ones, upper, preferred_element_type=jnp.float32)
+            rank = jnp.where(chose, rank, -100.0)
+            row = lax.broadcasted_iota(jnp.int32, (mine, 32, rows), 1) + (window(chip) - CAP * src)
+            hit = row.astype(jnp.float32) == rank[:, None, :]
+            one = jnp.where(hit, 1.0, 0.0).reshape(mine * 32, rows)
+            select[chip, :, core * rows : (core + 1) * rows] = one.astype(jnp.bfloat16)
+            weight = jnp.where(hit, note[:, None, :], 0.0).reshape(mine * 32, rows)
+            total = total + jnp.sum(weight, axis=1, keepdims=True)
+        gate[chip] = jnp.broadcast_to(total, (mine * 32, LANES))
+
+    def expand(chip, start, wide):
         cols = pl.ds(start, wide)
-        win = pl.ds(pl.multiple_of(window(src), 16), 32)
-        got = jnp.dot(select[src], buf[src, :, cols], preferred_element_type=jnp.float32)
-        got = (got * gate[src][:, 0:1]).astype(jnp.bfloat16).reshape(mine, 32, wide)
+        win = pl.ds(pl.multiple_of(window(chip), 16), 32)
+        tok = buf[pl.ds(2 * chip, 2), :, cols].reshape(2 * rows, wide)
+        got = jnp.dot(select[chip], tok, preferred_element_type=jnp.float32)
+        got = (got * gate[chip][:, 0:1]).astype(jnp.bfloat16).reshape(mine, 32, wide)
         out_ref[:, win, cols] = out_ref[:, win, cols] + got
 
     def from_sibling(src, k):
@@ -234,31 +238,16 @@
         return buf.at[src, :, pl.ds(pl.multiple_of(k * span, LANES), span)]
 
     def fill_main(zs, line, first=0, stop=last):
-        @pl.loop(0, 2 * (stop - first))
-        def _(i):
-            k = first + i // 2
-            theirs = i % 2
-            src = at(zs, line, jnp.where(theirs == 1, cp, c))
-
-            @pl.when(theirs == 1)
-            def _():
-                from_sibling(src, k)
-
-            expand(src, pl.multiple_of(k * span, LANES), span)
+        @pl.loop(first, stop)
+        def _(k):
+            from_sibling(at(zs, line, cp), k)
+            expand(zs * 2 + line, pl.multiple_of(k * span, LANES), span)
 
     def fill_side(zs):
-        start, wide = chunks[last]
-
-        @pl.loop(0, 4)
-        def _(i):
-            theirs = i % 2
-            src = at(zs, i // 2, jnp.where(theirs == 1, cp, c))
-
-            @pl.when(theirs == 1)
-            def _():
-                arrived(src, last)
-
-            expand(src, start, wide)
+        @pl.loop(0, 2)
+        def _(line):
+            arrived(at(zs, line, cp), last)
+            expand(zs * 2 + line, *chunks[last])
 
     def fill_far(d, line, first=0, stop=last):
         @pl.loop(0, 2)
@@ -281,6 +270,12 @@
     for d in range(1, depth):
         for k in range(last):
             main_step(d, k)
+            if d == 2:
+                fill_main(z, y, k, k + 1)
+            if d == 3:
+                fill_main(z, yp, k, k + 1)
+                fill_far(1, y, k, k + 1)
+                fill_far(2, y, k, k + 1)
         if d == 1:
             other = at(z, yp, c)
             arrived(other, last)
@@ -291,27 +286,24 @@
             for o in range(1, n):
                 for note in note_of((me + o) % n, (me + n - o) % n):
                     note.wait()
-            pl.loop(0, n)(build)
-            fill_main(z, y)
-            fill_side(z)
+            pl.loop(0, n // 2)(build)
+            both = jnp.sum(stats[...], axis=0)
+            loss_ref[0] = jnp.sum(both[:, :EXPERTS] * both[:, EXPERTS:]) * scale
         else:
             side_step(d - 1)
             if d == 2:
+                fill_side(z)
                 for k in range(last):
                     across_step(0, k)
-                fill_far(1, y)
-                fill_main(z, yp)
-                fill_side_far(1)
-    for d in range(2, depth):
-        fill_far(d, y)
     for k in range(last):
         across_step(1, k)
     fill_far(1, yp)
+    fill_side_far(1)
     side_step(depth - 1)
+    for d in range(3, depth):
+        fill_far(d, y)
     for d in range(2, depth):
         fill_side_far(d)
-    both = jnp.sum(stats[...], axis=0)
-    loss_ref[0] = jnp.sum(both[:, :EXPERTS] * both[:, EXPERTS:]) * scale
     for d in range(2, depth):
         for k in range(last):
             across_step(d, k)
@@ -348,8 +340,8 @@
             pltpu.VMEM((n, mine, rows), jnp.float32),
             pltpu.VMEM((1, 2 * EXPERTS), jnp.float32),
             pltpu.VMEM((n, 1, 2 * EXPERTS), jnp.float32),
-            pltpu.VMEM((n, mine * 32, rows), jnp.bfloat16),
-            pltpu.VMEM((n, mine * 32, LANES), jnp.float32),
+            pltpu.VMEM((n // 2, mine * 32, 2 * rows), jnp.bfloat16),
+            pltpu.VMEM((n // 2, mine * 32, LANES), jnp.float32),
             dma((n, chunks, 4)),
             dma((n, chunks)),
             dma((2, n)),
@@ -357,7 +349,7 @@
             dma((2,)),
         ],
         compiler_params=pltpu.CompilerParams(
-            collective_id=0, has_side_effects=True, vmem_limit_bytes=40 * 2**20
+            collective_id=0, has_side_effects=True, vmem_limit_bytes=54 * 2**20 + 2**19
         ),
     )(tokens, router_weight, expert_ids.T)
 
@@ -404,7 +396,7 @@
         rows, width = tokens.shape
         gathered = n * rows * width * 2
         fits = gathered <= 24 * 2**20 and (EXPERTS // n) % 8 == 0 and rows == EXPERTS
-        if fits and n % 16 == 0 and width % (32 * LANES) == 0:
+        if fits and n == 16 and width % (32 * LANES) == 0:
             return on_device_kernels(n, tokens, router_weight, expert_ids)
         return on_device(tokens, router_weight, expert_ids)
 

time: 113 us -> 110 us (0.973)
  local copies, waits for them, and re-layouts: 6.87 us -> 3.74 us
    unnamed x7 -> x1, local copies, waits for them, and re-layouts: 6.87 us -> 3.74 us
where the time goes in v3:
time: 110 us; the launch traced here: 109 us
  Pallas kernels  103 us (94%)
  local copies, waits for them, and re-layouts  3.74 us (3%)
  between operations  2.33 us (2%)
    pallas_call x1, Pallas kernels, on_device_kernels(): pl.pallas_call(functools.partial(dispatch_kernel, n, scale), out_shape=(p...  103 us
    unnamed x1, local copies, waits for them, and re-layouts  3.74 us

profile of v3, /device:TPU:1, one launch (start us, length us, event | category | flops | bytes accessed | tf_op | source)
XLA Modules:
  0.0 109.2 jit_solution(2756229768737554486)
XLA Ops:
  0.6 103.1 %shard_map.50 = (bf16[8,144,4096]{2,1,0:T(8,128)(2,1)S(1)}, f32[1]{0:T(128)}) custom-call(bf16[128,4096]{1,0:T(8,128)(2,1)} %x_hbm.1, bf16[4096,128]{1,0:T(8,128)(2,1)} %w_hbm.1, s32[8,128]{1,0:T(8,128)} %bitcast.1), custom_call_target="tpu_custom_call" | custom-call | tf_op jit(solution)/shard_map/pallas_call | solution.py:328
  103.8 3.7 %copy.7 = bf16[8,144,4096]{2,1,0:T(8,128)(2,1)} copy(bf16[8,144,4096]{2,1,0:T(8,128)(2,1)S(1)} %get-tuple-element.2) | data formatting | bytes 18874368
